TPU v7x, 32 devices: a whole 2x2x4 slice. The times are simulated.
32 devices in a mesh: row: 8 (over z, core), col: 4 (over y, x).
Axes of the slice: x: 2, y: 2, z: 4, core: 2. Of those that a mesh axis runs over, the one named last changes fastest.
Arguments:
- x_fwd: bfloat16 [512, 6144], P('row', 'col'), may hold values from -6 to 6
- x_bwd: bfloat16 [512, 6144], P('row', 'col'), may hold values from -6 to 6
- grad_out: bfloat16 [512, 6144], P('row', 'col'), may hold values from -1.5 to 1.5
- gain: float32 [6144], P('col'), may hold values from 0.1 to 1.9
- w_up: bfloat16 [6144, 12288], P('col', 'row'), may hold values from -0.078125 to 0.078125
- w_down: bfloat16 [12288, 6144], P('row', 'col'), may hold values from -0.0546875 to 0.0546875
Outputs:
- y_fwd: bfloat16 [512, 6144], P('row', 'col')
- dx_bwd: bfloat16 [512, 6144], P('row', 'col')
- step_up: float32 [6144, 12288], P('col', 'row')
- step_down: float32 [12288, 6144], P('row', 'col')
- step_gain: float32 [6144], P('col')
- grad_rms: float32 [], replicated
All inputs are finite; a program needn't handle non-finite values.
Results may differ from a plain program's by a relative error of at most 0.0017.
The roundings to bfloat16 on the way count: a program that leaves them out, or rounds other values in their place, can miss the bound.
Values may be sent and summed in bfloat16 or wider, within the bound.
A program may use at most 128 MiB of HBM per device.

v0:
```python
import math

import jax
import jax.numpy as jnp
from jax import lax
from jax.sharding import PartitionSpec as P

D = 6144
FF = 12288


eps = 1e-06
clip_share = 0.25


def erf_gelu(value):
    return 0.5 * value * (1.0 + lax.erf(value * 0.7071067811865476))


def gelu_slope(value):
    return (
        0.5 * (1.0 + lax.erf(value * 0.7071067811865476))
        + value * jnp.exp(-0.5 * value * value) * 0.3989422804014327
    )


def contract(left, right, left_dim, right_dim):
    return lax.dot_general(
        left, right, (((left_dim,), (right_dim,)), ((), ())), preferred_element_type=jnp.float32
    )


def row_sums(tokens):
    values = tokens.astype(jnp.float32)
    return (jnp.sum(values, -1), jnp.sum(values * values, -1))


def normalize(tokens, first, second):
    values = tokens.astype(jnp.float32)
    centre = first / D
    spread = second / D - centre * centre
    inv_scale = lax.rsqrt(spread + eps)
    return ((values - centre[:, None]) * inv_scale[:, None], inv_scale)


def up_both(normed_a, normed_b, w_up):
    full_a, full_b = (
        lax.all_gather(normed_a, "row", axis=0, tiled=True),
        lax.all_gather(normed_b, "row", axis=0, tiled=True),
    )
    width = w_up.shape[1]
    summed = lax.psum_scatter(
        jnp.concatenate(
            [
                jnp.dot(full_a, w_up, preferred_element_type=jnp.float32),
                jnp.dot(full_b, w_up, preferred_element_type=jnp.float32),
            ],
            1,
        ),
        "col",
        scatter_dimension=0,
        tiled=True,
    )
    return (summed[:, :width], summed[:, width:], full_b)


def on_device(x_fwd, x_bwd, grad_out, gain, w_up, w_down):
    first_a, second_a = row_sums(x_fwd)
    first_b, second_b = row_sums(x_bwd)
    first_a, second_a, first_b, second_b = lax.psum((first_a, second_a, first_b, second_b), "col")
    centred_a, _ = normalize(x_fwd, first_a, second_a)
    centred_b, inv_scale = normalize(x_bwd, first_b, second_b)
    normed_a = (centred_a * gain).astype(jnp.bfloat16)
    normed_b = (centred_b * gain).astype(jnp.bfloat16)
    pre_a, pre_b, normed_full = up_both(normed_a, normed_b, w_up)
    hidden_a = erf_gelu(pre_a).astype(jnp.bfloat16)
    output_part = jnp.dot(
        lax.all_gather(hidden_a, "col", axis=0, tiled=True),
        w_down,
        preferred_element_type=jnp.float32,
    )
    output_sum = lax.psum_scatter(output_part, "row", scatter_dimension=0, tiled=True)
    y_fwd = (x_fwd.astype(jnp.float32) + output_sum).astype(jnp.bfloat16)
    hidden_b = erf_gelu(pre_b).astype(jnp.bfloat16)
    grad_full = lax.all_gather(grad_out, "row", axis=0, tiled=True)
    grad_hidden = lax.psum_scatter(
        contract(grad_full, w_down, 1, 1), "col", scatter_dimension=0, tiled=True
    )
    grad_pre = (grad_hidden * gelu_slope(pre_b)).astype(jnp.bfloat16)
    hidden_piece = lax.all_gather(hidden_b, "col", axis=0, tiled=True)
    pre_piece = lax.all_gather(grad_pre, "col", axis=0, tiled=True)
    down_total = contract(hidden_piece, grad_full, 0, 0)
    up_total = contract(normed_full, pre_piece, 0, 0)
    input_total = contract(pre_piece, w_up, 1, 1)
    grad_normed = lax.psum_scatter(input_total, "row", scatter_dimension=0, tiled=True)
    scaled = grad_normed * gain
    first_back = jnp.sum(scaled, -1)
    second_back = jnp.sum(scaled * centred_b, -1)
    first_back, second_back = lax.psum((first_back, second_back), "col")
    dx_bwd = (
        grad_out.astype(jnp.float32)
        + inv_scale[:, None]
        * (scaled - first_back[:, None] / D - centred_b * (second_back[:, None] / D))
    ).astype(jnp.bfloat16)
    gain_part = jnp.sum(grad_normed * centred_b, 0)
    weight_squares = jnp.sum(up_total * up_total) + jnp.sum(down_total * down_total)
    g_gain = lax.psum(gain_part, "row")
    first_row = (lax.axis_index("row") == 0).astype(jnp.float32)
    total = lax.psum(weight_squares + first_row * jnp.sum(g_gain * g_gain), ("row", "col"))
    param_count = 2 * D * FF + D
    norm_value = jnp.sqrt(total)
    grad_rms = norm_value / math.sqrt(param_count)
    factor = jnp.minimum(1.0, clip_share * math.sqrt(param_count) / norm_value)
    return (y_fwd, dx_bwd, up_total * factor, down_total * factor, g_gain * factor, grad_rms)


def solution(mesh):
    placed = (
        P("row", "col"),
        P("row", "col"),
        P("row", "col"),
        P("col"),
        P("col", "row"),
        P("row", "col"),
    )
    return jax.shard_map(
        on_device,
        mesh=mesh,
        in_specs=placed,
        out_specs=(
            P("row", "col"),
            P("row", "col"),
            P("col", "row"),
            P("row", "col"),
            P("col"),
            P(),
        ),
        check_vma=False,
    )
```

profile of v0, /device:TPU:0, one launch (start us, length us, event | category | flops | bytes accessed | tf_op | source)
XLA Modules:
  0.0 446.6 jit_solution(12459251885347289089)
XLA Ops:
  7.2 0.0 all-gather.13.cloned.1.call-start
  7.2 0.7 all-gather.13.cloned.1.call-update
  7.9 0.0 all-gather.7.cloned.1.call-start
  7.9 1.1 convert_reduce_fusion
  9.0 1.1 convert_reduce_fusion.1
  10.1 11.4 %all-reduce.1 = (f32[64]{0:T(128)S(1)}, f32[64]{0:T(128)S(1)}, f32[64]{0:T(128)S(1)}, f32[64]{0:T(128)S(1)}) all-reduce(f32[64]{0:T(128)S(1)} %get-tuple-element.12, f32[64]{0:T(128)S(1)} %get-tuple-element.11, f32[64]{0:T(128)S(1)} %get-tuple-element.10, f32[64]{0:T(128)S(1)} %get-tuple-element.9), channel_id=1, replica_groups=mesh['row'=8,'col'=4] {'col'}, use_global_device_ids=true, to_apply=%region_7.0 | all-reduce | flops 256 | bytes 2048 | tf_op jit(solution)/shard_map/psum | solution.py:70
  21.5 2.0 fusion.21
  23.6 0.0 all-gather.7.cloned.1.call-update
  23.6 0.0 all-gather.9.cloned.1.call-start
  23.6 0.7 all-gather.9.cloned.1.call-update
  24.3 0.0 reduce-scatter.9.cloned.1.call-start
  24.4 13.3 %all-gather.13.cloned.1.call-done = bf16[512,1536]{1,0:T(8,128)(2,1)} async-done(((bf16[64,1536]{1,0:T(8,128)(2,1)}), bf16[512,1536]{1,0:T(8,128)(2,1)}) %all-gather.13.cloned.1.call-update) | async-done | bytes 1572880 | tf_op jit(solution)/shard_map/all_gather | solution.py:85
  37.6 7.1 %fusion.27 = f32[512,1536]{1,0:T(8,128)} fusion(bf16[512,1536]{1,0:T(8,128)(2,1)} %all-gather.13.cloned.1.call-done, bf16[1536,1536]{1,0:T(8,128)(2,1)} %param.11), kind=kOutput, calls=%fused_computation.52 | convolution fusion | flops 2415919104 | bytes 9437184 | tf_op jit(solution)/shard_map/dot_general | solution.py:28
  44.8 0.0 reduce-scatter.9.cloned.1.call-update
  44.8 0.0 reduce-scatter.5.cloned.1.call-start
  44.8 19.4 %all-gather.7.cloned.1.call-done = bf16[512,1536]{1,0:T(8,128)(2,1)} async-done(((bf16[64,1536]{1,0:T(8,128)(2,1)}), bf16[512,1536]{1,0:T(8,128)(2,1)}) %all-gather.7.cloned.1.call-update) | async-done | bytes 1572880 | tf_op jit(solution)/shard_map/all_gather | solution.py:48
  64.3 4.9 %fusion.24 = f32[512,1536]{1,0:T(8,128)S(1)} fusion(bf16[512,1536]{1,0:T(8,128)(2,1)} %all-gather.7.cloned.1.call-done, bf16[1536,1536]{1,0:T(8,128)(2,1)} %param.10), kind=kOutput, calls=%fused_computation.49 | convolution fusion | flops 2415919104 | bytes 9437184 | tf_op jit(solution)/shard_map/dot_general | solution.py:55
  69.2 21.7 %all-gather.9.cloned.1.call-done = bf16[512,1536]{1,0:T(8,128)(2,1)} async-done(((bf16[64,1536]{1,0:T(8,128)(2,1)}), bf16[512,1536]{1,0:T(8,128)(2,1)}) %all-gather.9.cloned.1.call-update) | async-done | bytes 1572880 | tf_op jit(solution)/shard_map/all_gather | solution.py:49
  90.9 4.9 %fusion.25 = f32[512,1536]{1,0:T(8,128)S(1)} fusion(bf16[512,1536]{1,0:T(8,128)(2,1)} %all-gather.9.cloned.1.call-done, bf16[1536,1536]{1,0:T(8,128)(2,1)} %param.10), kind=kOutput, calls=%fused_computation.50 | convolution fusion | flops 2415919104 | bytes 9437184 | tf_op jit(solution)/shard_map/dot_general | solution.py:56
  95.9 3.3 pad_maximum_fusion
  99.1 0.0 reduce-scatter.5.cloned.1.call-update
  99.1 0.0 all-gather.15.cloned.1.call-start
  99.2 38.2 %reduce-scatter.9.cloned.1.call-done = f32[128,1536]{1,0:T(8,128)} async-done(((f32[512,1536]{1,0:T(8,128)}), f32[128,1536]{1,0:T(8,128)}) %reduce-scatter.9.cloned.1.call-update) | async-done | bytes 786448 | tf_op jit(solution)/shard_map/reduce_scatter | solution.py:86
  137.4 73.5 %reduce-scatter.5.cloned.1.call-done = f32[128,3072]{1,0:T(8,128)} async-done(((f32[512,3072]{1,0:T(8,128)}), f32[128,3072]{1,0:T(8,128)}) %reduce-scatter.5.cloned.1.call-update) | async-done | bytes 1572880 | tf_op jit(solution)/shard_map/reduce_scatter | solution.py:52
  210.9 3.0 multiply_convert_fusion
  213.9 0.0 all-gather.15.cloned.1.call-update
  213.9 0.0 all-gather.11.cloned.1.call-start
  214.0 0.7 all-gather.11.cloned.1.call-update
  214.7 0.0 all-gather.17.cloned.1.call-start
  214.7 0.7 all-gather.17.cloned.1.call-update
  215.4 0.0 reduce-scatter.11.cloned.1.call-start
  215.5 29.5 %all-gather.15.cloned.1.call-done = bf16[512,1536]{1,0:T(8,128)(2,1)} async-done(((bf16[128,1536]{1,0:T(8,128)(2,1)}), bf16[512,1536]{1,0:T(8,128)(2,1)}) %all-gather.15.cloned.1.call-update) | async-done | bytes 1572880 | tf_op jit(solution)/shard_map/all_gather | solution.py:91
  244.9 7.1 %fusion.28 = f32[512,1536]{1,0:T(8,128)} fusion(bf16[512,1536]{1,0:T(8,128)(2,1)} %all-gather.15.cloned.1.call-done, bf16[1536,1536]{1,0:T(8,128)(2,1)} %param.10), kind=kOutput, calls=%fused_computation.53 | convolution fusion | flops 2415919104 | bytes 9437184 | tf_op jit(solution)/shard_map/dot_general | solution.py:28
  252.0 0.0 reduce-scatter.11.cloned.1.call-update
  252.1 0.2 reduce-scatter.7.cloned.1.call-start
  252.3 25.3 %all-gather.11.cloned.1.call-done = bf16[512,1536]{1,0:T(8,128)(2,1)} async-done(((bf16[128,1536]{1,0:T(8,128)(2,1)}), bf16[512,1536]{1,0:T(8,128)(2,1)}) %all-gather.11.cloned.1.call-update) | async-done | bytes 1572880 | tf_op jit(solution)/shard_map/all_gather | solution.py:78
  277.6 7.1 %fusion.26 = f32[512,1536]{1,0:T(8,128)} fusion(bf16[512,1536]{1,0:T(8,128)(2,1)} %all-gather.11.cloned.1.call-done, bf16[1536,1536]{1,0:T(8,128)(2,1)} %param.11), kind=kOutput, calls=%fused_computation.51 | convolution fusion | flops 2415919104 | bytes 9437184 | tf_op jit(solution)/shard_map/dot_general | solution.py:77
  284.8 0.0 reduce-scatter.7.cloned.1.call-update
  284.8 1.4 copy-done.5
  286.2 0.5 copy-done.6
  286.7 6.0 %multiply_reduce_fusion.1 = (f32[]{:T(128)}, f32[1536,1536]{1,0:T(8,128)}) fusion(bf16[512,1536]{1,0:T(8,128)(2,1)S(1)} %copy-done.5, bf16[512,1536]{1,0:T(8,128)(2,1)S(1)} %copy-done.6), kind=kOutput, calls=%fused_computation.1 | convolution fusion | flops 2420637696 | bytes 12582916 | tf_op jit(solution)/shard_map/dot_general | solution.py:28
  292.7 18.2 %all-gather.17.cloned.1.call-done = bf16[512,1536]{1,0:T(8,128)(2,1)} async-done(((bf16[128,1536]{1,0:T(8,128)(2,1)}), bf16[512,1536]{1,0:T(8,128)(2,1)}) %all-gather.17.cloned.1.call-update) | async-done | bytes 1572880 | tf_op jit(solution)/shard_map/all_gather | solution.py:90
  310.9 8.9 %multiply_reduce_fusion = (f32[]{:T(128)}, f32[1536,1536]{1,0:T(8,128)}) fusion(bf16[512,1536]{1,0:T(8,128)(2,1)} %all-gather.17.cloned.1.call-done, bf16[512,1536]{1,0:T(8,128)(2,1)} %all-gather.13.cloned.1.call-done), kind=kOutput, calls=%fused_computation | convolution fusion | flops 2420637696 | bytes 12582916 | tf_op jit(solution)/shard_map/dot_general | solution.py:28
  321.1 32.5 %reduce-scatter.11.cloned.1.call-done = f32[64,1536]{1,0:T(8,128)} async-done(((f32[512,1536]{1,0:T(8,128)}), f32[64,1536]{1,0:T(8,128)}) %reduce-scatter.11.cloned.1.call-update) | async-done | bytes 393232 | tf_op jit(solution)/shard_map/reduce_scatter | solution.py:95
  353.6 0.0 copy-done
  353.6 0.0 copy-done.4
  353.6 1.4 fusion.17
  355.0 16.1 %psum.62 = f32[1536]{0:T(1024)S(1)} all-reduce(f32[1536]{0:T(1024)S(1)} %get-tuple-element.6), channel_id=1, replica_groups=mesh['row'=8,'col'=4] {'row'}, use_global_device_ids=true, to_apply=%region_19.0 | all-reduce | flops 1536 | bytes 12288 | tf_op jit(solution)/shard_map/psum | solution.py:107
  371.1 0.6 multiply_reduce_fusion.3
  372.3 38.8 %psum.63 = f32[]{:T(128)} all-reduce(f32[]{:T(128)S(6)} %add.60), channel_id=1, replica_groups=mesh['row'=8,'col'=4] {'row','col'}, use_global_device_ids=true, to_apply=%region_21.0 | all-reduce | flops 1 | bytes 8 | tf_op jit(solution)/shard_map/psum | solution.py:109
  411.9 9.9 %all-reduce = (f32[64]{0:T(128)S(1)}, f32[64]{0:T(128)S(1)}) all-reduce(f32[64]{0:T(128)S(1)} %get-tuple-element.7, f32[64]{0:T(128)S(1)} %get-tuple-element.8), channel_id=1, replica_groups=mesh['row'=8,'col'=4] {'col'}, use_global_device_ids=true, to_apply=%region_15.0 | all-reduce | flops 128 | bytes 1024 | tf_op jit(solution)/shard_map/psum | solution.py:99
  421.8 0.6 broadcast_multiply_fusion.2
  422.5 8.7 %broadcast_multiply_fusion = f32[1536,1536]{1,0:T(8,128)} fusion(f32[1536,1536]{1,0:T(8,128)} %get-tuple-element.31, f32[]{:T(128)S(6)} %min.3), kind=kLoop, calls=%fused_computation.3 | loop fusion | flops 2359296 | bytes 18874372 | tf_op jit(solution)/shard_map/mul | solution.py:114
  431.1 0.0 slice-done
  431.1 0.0 slice-done.1
  431.1 0.0 slice-done.2
  431.1 0.0 copy-start.1
  431.2 0.0 copy-start.2
  431.2 0.0 copy-start.3
  431.2 4.8 %broadcast_multiply_fusion.1 = f32[1536,1536]{1,0:T(8,128)} fusion(f32[1536,1536]{1,0:T(8,128)S(1)} %bitcast.15, f32[]{:T(128)S(6)} %min.3), kind=kLoop, calls=%fused_computation.4 | loop fusion | flops 2359296 | bytes 18874372 | tf_op jit(solution)/shard_map/mul | solution.py:114
  436.0 0.0 copy-done.1
  436.0 1.7 fusion.23
  437.7 0.0 copy-done.2
  437.7 0.9 fusion.16
  (13 shorter events, 0.0 us)
Async XLA Ops:
  7.2 30.5 %all-gather.13.cloned.1.call-start = ((), (), s32[]{:S(2)}) async-start(), calls=%async_computation.9 | async-start | bytes 1769472 | tf_op jit(solution)/shard_map/all_gather | solution.py:85
  7.9 56.4 %all-gather.7.cloned.1.call-start = ((), (), s32[]{:S(2)}) async-start(), calls=%async_computation.4 | async-start | bytes 1769472 | tf_op jit(solution)/shard_map/all_gather | solution.py:48
  23.6 67.3 %all-gather.9.cloned.1.call-start = ((), (), s32[]{:S(2)}) async-start(), calls=%async_computation.5 | async-start | bytes 1769472 | tf_op jit(solution)/shard_map/all_gather | solution.py:49
  24.3 113.1 %reduce-scatter.9.cloned.1.call-start = ((), (), s32[]{:S(2)}) async-start(), calls=%async_computation.10 | async-start | bytes 3932160 | tf_op jit(solution)/shard_map/reduce_scatter | solution.py:86
  44.8 166.1 %reduce-scatter.5.cloned.1.call-start = ((), (), s32[]{:S(2)}) async-start(), calls=%async_computation.6 | async-start | bytes 7864320 | tf_op jit(solution)/shard_map/reduce_scatter | solution.py:52
  99.1 145.8 %all-gather.15.cloned.1.call-start = ((), (), s32[]{:S(2)}) async-start(), calls=%async_computation.11 | async-start | bytes 1966080 | tf_op jit(solution)/shard_map/all_gather | solution.py:91
  213.9 63.7 %all-gather.11.cloned.1.call-start = ((), (), s32[]{:S(2)}) async-start(), calls=%async_computation.7 | async-start | bytes 1966080 | tf_op jit(solution)/shard_map/all_gather | solution.py:78
  214.7 96.2 %all-gather.17.cloned.1.call-start = ((), (), s32[]{:S(2)}) async-start(), calls=%async_computation.13 | async-start | bytes 1966080 | tf_op jit(solution)/shard_map/all_gather | solution.py:90
  215.4 138.2 %reduce-scatter.11.cloned.1.call-start = ((), (), s32[]{:S(2)}) async-start(), calls=%async_computation.12 | async-start | bytes 3538944 | tf_op jit(solution)/shard_map/reduce_scatter | solution.py:95
  252.1 183.9 %reduce-scatter.7.cloned.1.call-start = ((), (), s32[]{:S(2)}) async-start(), calls=%async_computation.8 | async-start | bytes 3538944 | tf_op jit(solution)/shard_map/reduce_scatter | solution.py:82
  284.8 1.4 copy-start.5
  284.8 1.9 copy-start.6
  292.7 60.9 %copy-start = (bf16[64,1536]{1,0:T(8,128)(2,1)S(1)}, bf16[64,1536]{1,0:T(8,128)(2,1)}, u32[]{:S(2)}) copy-start(bf16[64,1536]{1,0:T(8,128)(2,1)} %param.7) | copy-start | bytes 589828
  292.7 60.9 %copy-start.4 = (f32[1536]{0:T(1024)S(1)}, f32[1536]{0:T(1024)}, u32[]{:S(2)}) copy-start(f32[1536]{0:T(1024)} %param.9) | copy-start | bytes 18436
  353.6 77.5 %slice-start = ((s8[9437184]{0:T(1024)(128)(4,1)}), s8[1048576]{0:T(1024)(128)(4,1)S(1)}, s32[]{:S(2)}) async-start(s8[9437184]{0:T(1024)(128)(4,1)} %bitcast.14), calls=%async_computation.14 | async-start | bytes 2097152
  422.4 8.7 %slice-start.1 = ((s8[9437184]{0:T(1024)(128)(4,1)}), s8[4194304]{0:T(1024)(128)(4,1)S(1)}, s32[]{:S(2)}) async-start(s8[9437184]{0:T(1024)(128)(4,1)} %bitcast.14), calls=%async_computation.15 | async-start | bytes 8388608
  422.4 8.7 %slice-start.2 = ((s8[9437184]{0:T(1024)(128)(4,1)}), s8[4194304]{0:T(1024)(128)(4,1)S(1)}, s32[]{:S(2)}) async-start(s8[9437184]{0:T(1024)(128)(4,1)} %bitcast.14), calls=%async_computation.16 | async-start | bytes 8388608
  431.1 4.8 %copy-start.1 = (bf16[64,1536]{1,0:T(8,128)(2,1)S(1)}, bf16[64,1536]{1,0:T(8,128)(2,1)}, u32[]{:S(2)}) copy-start(bf16[64,1536]{1,0:T(8,128)(2,1)} %param.6) | copy-start | bytes 589828
  431.2 6.5 %copy-start.2 = (f32[64,1536]{1,0:T(8,128)S(1)}, f32[64,1536]{1,0:T(8,128)}, u32[]{:S(2)}) copy-start(f32[64,1536]{1,0:T(8,128)} %reduce-scatter.11.cloned.1.call-done) | copy-start | bytes 1179652
  431.2 6.5 %copy-start.3 = (bf16[64,1536]{1,0:T(8,128)(2,1)S(1)}, bf16[64,1536]{1,0:T(8,128)(2,1)}, u32[]{:S(2)}) copy-start(bf16[64,1536]{1,0:T(8,128)(2,1)} %param.8) | copy-start | bytes 589828
Sparse Core Ops, SparseCore 0:
  9.6 27.9 all-gather.12
  39.8 24.3 all-gather.6
  66.5 24.3 all-gather.8
  94.3 43.0 reduce-scatter.8
  140.8 70.0 reduce-scatter.4
  214.0 30.8 all-gather.14
  246.8 30.8 all-gather.10
  280.0 30.8 all-gather.16
  313.2 40.3 reduce-scatter.10
  355.8 40.2 reduce-scatter.6
where the time goes:
time: 447 us
  waiting for transfers between devices  274 us (61%)
  blocking collectives  76.2 us (17%)
  matrix products  46.1 us (10%)
  other arithmetic  29.2 us (7%)
  between operations  18.1 us (4%)
    reduce_scatter x1, waiting for transfers between devices, up_both(): lax.psum_scatter(jnp.concatenate([jnp.dot(full_a, w_up, preferred_element...  73.5 us
    psum x1, blocking collectives, on_device(): lax.psum(weight_squares + first_row * jnp.sum(g_gain * g_gain), ('row', '...  38.8 us
    reduce_scatter x1, waiting for transfers between devices, on_device(): lax.psum_scatter(contract(grad_full, w_down, 1, 1), 'col', scatter_dimens...  38.2 us
    reduce_scatter x1, waiting for transfers between devices, on_device(): lax.psum_scatter(input_total, 'row', scatter_dimension=0, tiled=True)  32.5 us
    all_gather x1, waiting for transfers between devices, on_device(): pre_piece = lax.all_gather(grad_pre, 'col', axis=0, tiled=True)  29.5 us
    dot_general x4, matrix products, contract(): lax.dot_general(left, right, (((left_dim,), (right_dim,)), ((), ())), pre...  29.2 us
    all_gather x1, waiting for transfers between devices, on_device(): lax.all_gather(hidden_a, 'col', axis=0, tiled=True)  25.3 us
    all_gather x1, waiting for transfers between devices, up_both(): lax.all_gather(normed_b, 'row', axis=0, tiled=True)  21.7 us
  transfers between devices with their start and end apart: 10, of which 9 were waited for; matrix products, arithmetic and copies ran while one was open for 16% of the time, Pallas kernels for 0%

commit v1 on v0

--- a/solution.py
+++ b/solution.py
@@ -1,8 +1,11 @@
+import functools
 import math
 
 import jax
 import jax.numpy as jnp
 from jax import lax
+from jax.experimental import pallas as pl
+from jax.experimental.pallas import tpu as pltpu
 from jax.sharding import PartitionSpec as P
 
 D = 6144
@@ -114,6 +117,536 @@
     return (y_fwd, dx_bwd, up_total * factor, down_total * factor, g_gain * factor, grad_rms)
 
 
+MESH = pl.DeviceIdType.MESH
+VMEM = pl.BlockSpec(memory_space=pltpu.VMEM)
+F32 = jnp.float32
+BF16 = jnp.bfloat16
+DMA = pltpu.SemaphoreType.DMA
+GRANT = 60 * 1024 * 1024
+
+
+def greet(peers):
+    barrier = pltpu.get_barrier_semaphore()
+    for peer in peers:
+        pl.semaphore_signal(barrier, inc=1, device_id=peer, device_id_type=MESH)
+    pl.semaphore_wait(barrier, len(peers))
+
+
+def send(src, dst, send_sem, recv_sem, peer):
+    return pltpu.make_async_remote_copy(
+        src_ref=src, dst_ref=dst, send_sem=send_sem, recv_sem=recv_sem,
+        device_id=peer, device_id_type=MESH,
+    )
+
+
+def arrived(ref, sem, peer):
+    pltpu.make_async_remote_copy(
+        src_ref=ref, dst_ref=ref, send_sem=sem, recv_sem=sem,
+        device_id=peer, device_id_type=MESH,
+    ).wait_recv()
+
+
+def greet_line(line, chip, chips, others):
+    barrier = pltpu.get_barrier_semaphore()
+    for peer in others:
+        pl.semaphore_signal(barrier, inc=1, device_id=peer, device_id_type=MESH)
+
+    @pl.when(chip > 0)
+    def _():
+        pl.semaphore_signal(barrier, inc=1, device_id=line(-1), device_id_type=MESH)
+
+    @pl.when(chip < chips - 1)
+    def _():
+        pl.semaphore_signal(barrier, inc=1, device_id=line(1), device_id_type=MESH)
+
+    beside = jnp.minimum(chip, 1) + jnp.minimum(chips - 1 - chip, 1)
+    pl.semaphore_wait(barrier, len(others) + beside)
+
+
+def normal_of(values, stats, at, width):
+    centre = stats[:, at : at + 1] / width
+    spread = stats[:, at + 1 : at + 2] / width - centre * centre
+    inv = lax.rsqrt(spread + eps)
+    return (values - centre) * inv, inv
+
+
+def lanes_of(columns):
+    rows = columns[0].shape[0]
+    lane = lax.broadcasted_iota(jnp.int32, (rows, 128), 1)
+    out = jnp.zeros((rows, 128), F32)
+    for i, column in enumerate(columns):
+        out = jnp.where(lane == i, column, out)
+    return out
+
+
+def gather_kernel(R, C, width, xa, xb, go, gain, full, stats, st_own, st_in,
+                  st_send, st_recv, s_right, s_left, s_sib, recv):
+    row, col = lax.axis_index("row"), lax.axis_index("col")
+    chips = R // 2
+    chip, core = row // 2, row % 2
+    sib = {"row": row + 1 - 2 * core, "col": col}
+
+    def line(step):
+        return {"row": row + 2 * step, "col": col}
+
+    cols = [{"row": row, "col": (col + i) % C} for i in range(1, C)]
+    greet_line(line, chip, chips, cols + [sib])
+
+    def spread(j, owner, slot, src, to_right, to_left):
+        dst = full.at[j, owner]
+        out = [(None, send(src, dst, s_sib.at[j, slot], recv.at[j, owner], sib))]
+        if to_right:
+            out.append((chip < chips - 1,
+                        send(src, dst, s_right.at[j, slot], recv.at[j, owner], line(1))))
+        if to_left:
+            out.append((chip > 0,
+                        send(src, dst, s_left.at[j, slot], recv.at[j, owner], line(-1))))
+        return out
+
+    def start(copies):
+        for cond, copy in copies[::-1]:
+            if cond is None:
+                copy.start()
+            else:
+                pl.when(cond)(copy.start)
+
+    def finish(copies):
+        for cond, copy in copies:
+            if cond is None:
+                copy.wait_send()
+            else:
+                pl.when(cond)(copy.wait_send)
+
+    own = {2: spread(2, row, 0, go, True, True)}
+    start(own[2])
+    a, b = xa[...].astype(F32), xb[...].astype(F32)
+    sums = []
+    for v in (a, b):
+        sums += [jnp.sum(v, 1, keepdims=True), jnp.sum(v * v, 1, keepdims=True)]
+    st_own[...] = lanes_of(sums)
+    st_copies = [send(st_own, st_in.at[i], st_send.at[i], st_recv.at[i], p)
+                 for i, p in enumerate(cols)]
+    for copy in st_copies:
+        copy.start()
+    full[2, row] = go[...]
+    for copy in st_copies:
+        copy.wait()
+    total = st_own[...]
+    for i in range(C - 1):
+        total = total + st_in[i]
+    stats[...] = total
+    for j, x, at in ((1, xb, 2), (0, xa, 0)):
+        hat, _ = normal_of(x[...].astype(F32), total, at, width)
+        full[j, row] = (hat * gain[...]).astype(BF16)
+        own[j] = spread(j, row, 0, full.at[j, row], True, True)
+        start(own[j])
+    for step in range(1, chips):
+        for j in (2, 1, 0):
+            for sign in (-1, 1):
+                ok = chip >= step if sign < 0 else chip + step < chips
+
+                @pl.when(ok)
+                def _():
+                    owner = row + 2 * sign * step
+                    arrived(full.at[j, owner], recv.at[j, owner], line(sign))
+                    slot = step if sign < 0 else chips - 1 + step
+                    start(spread(j, owner, slot, full.at[j, owner], sign < 0, sign > 0))
+    for j in (2, 1, 0):
+        finish(own[j])
+        for chip_of in range(chips):
+            owner = 2 * chip_of + 1 - core
+            arrived(full.at[j, owner], recv.at[j, owner], sib)
+    for step in range(1, chips):
+        for j in (2, 1, 0):
+            for sign in (-1, 1):
+                ok = chip >= step if sign < 0 else chip + step < chips
+
+                @pl.when(ok)
+                def _():
+                    owner = row + 2 * sign * step
+                    slot = step if sign < 0 else chips - 1 + step
+                    finish(spread(j, owner, slot, full.at[j, owner], sign < 0, sign > 0))
+
+
+def gather_rows(R, C, width, x_fwd, x_bwd, grad_out, gain):
+    rows, columns = x_fwd.shape
+    slots = 2 * (R // 2) - 1
+    return pl.pallas_call(
+        functools.partial(gather_kernel, R, C, width),
+        out_shape=(jax.ShapeDtypeStruct((3, R, rows, columns), BF16),
+                   jax.ShapeDtypeStruct((rows, 128), F32)),
+        in_specs=[VMEM] * 4,
+        out_specs=(VMEM, VMEM),
+        scratch_shapes=[
+            pltpu.VMEM((rows, 128), F32), pltpu.VMEM((C - 1, rows, 128), F32),
+            DMA((C - 1,)), DMA((C - 1,)),
+            DMA((3, slots)), DMA((3, slots)), DMA((3, slots)), DMA((3, R)),
+        ],
+        compiler_params=pltpu.CompilerParams(
+            collective_id=0, has_side_effects=True, vmem_limit_bytes=GRANT),
+        cost_estimate=pl.CostEstimate(flops=10**9, bytes_accessed=10**7, transcendentals=0),
+    )(x_fwd, x_bwd, grad_out, gain)
+
+
+def middle_kernel(full, w_up, w_down, out, out_send, buf, inb, own, sem_s, sem_r, g_s, g_r):
+    row, col = lax.axis_index("row"), lax.axis_index("col")
+    flip_x = col + 1 - 2 * (col % 2)
+    flip_y = (col + 2) % 4
+    diag = 3 - col
+    peer_x, peer_y = {"row": row, "col": flip_x}, {"row": row, "col": flip_y}
+    greet([peer_x, peer_y])
+    tokens, wide = out.shape[2], out.shape[3]
+    half = wide // 2
+    tile = half // 2
+
+    def part(j, q, put):
+        @pl.loop(0, wide // tile)
+        def _(t):
+            at = pl.ds(pl.multiple_of(t * tile, tile), tile)
+            left = full[j, q]
+            if j == 2:
+                piece = lax.dot_general(left, w_down[at, :], (((1,), (1,)), ((), ())),
+                                        preferred_element_type=F32)
+            else:
+                piece = jnp.dot(left, w_up[:, at], preferred_element_type=F32)
+            put(t, piece)
+
+    def into(j, base):
+        def put(t, piece):
+            buf[j, base + t // 2, :, pl.ds(pl.multiple_of((t % 2) * tile, tile), tile)] = piece
+        return put
+
+    def keep(j):
+        def put(t, piece):
+            own[j, t // 2, :, pl.ds(pl.multiple_of((t % 2) * tile, tile), tile)] = piece
+        return put
+
+    target = (peer_x, peer_y, peer_x, peer_x, peer_y, peer_y)
+
+    def copy(j, s):
+        return send(buf.at[j, s], inb.at[j, s], sem_s.at[j, s], sem_r.at[j, s], target[s])
+
+    def products(j):
+        part(j, diag, into(j, 0))
+        copy(j, 0).start()
+        copy(j, 1).start()
+        part(j, flip_x, into(j, 2))
+        copy(j, 2).start()
+        part(j, flip_y, into(j, 4))
+        copy(j, 5).start()
+        part(j, col, keep(j))
+
+    def transit(j):
+        copy(j, 0).wait_recv()
+        buf[j, 4] = buf[j, 4] + inb[j, 0]
+        copy(j, 4).start()
+        copy(j, 1).wait_recv()
+        buf[j, 3] = buf[j, 3] + inb[j, 1]
+        copy(j, 3).start()
+
+    def total(j):
+        for s in range(2, 6):
+            copy(j, s).wait_recv()
+
+    def summed(j, h, at):
+        return own[j, h, at, :] + inb[j, 2 + h, at, :] + inb[j, 4 + h, at, :]
+
+    chunk = 16
+
+    def over(body):
+        @pl.loop(0, tokens // chunk)
+        def _(i):
+            for h in range(2):
+                body(h, pl.ds(pl.multiple_of(i * chunk, chunk), chunk))
+
+    def first(k, which):
+        peer = (peer_x, peer_y)[which]
+        return send(out_send.at[k], out.at[k, col], g_s.at[k, which], g_r.at[k, which], peer)
+
+    def relay(k, which):
+        owner = (flip_x, flip_y)[which]
+        ref = out.at[k, owner, :, pl.ds(which * half, half)]
+        return send(ref, ref, g_s.at[k, 2 + which], g_r.at[k, 2 + which], (peer_y, peer_x)[which])
+
+    def publish(k):
+        first(k, 0).start()
+        first(k, 1).start()
+
+    def pass_on(k):
+        first(k, 0).wait_recv()
+        relay(k, 0).start()
+        first(k, 1).wait_recv()
+        relay(k, 1).start()
+
+    products(2)
+    products(1)
+    transit(2)
+    products(0)
+    transit(1)
+    total(2)
+    total(1)
+
+    def backward(h, at):
+        v = summed(1, h, at)
+        phi = 0.5 * (1.0 + lax.erf(v * 0.7071067811865476))
+        g = summed(2, h, at)
+        slope = phi + v * jnp.exp(-0.5 * v * v) * 0.3989422804014327
+        out_send[1, at, h * half : (h + 1) * half] = (v * phi).astype(BF16)
+        out_send[2, at, h * half : (h + 1) * half] = (g * slope).astype(BF16)
+
+    over(backward)
+    transit(0)
+    publish(2)
+    publish(1)
+    total(0)
+
+    def forward(h, at):
+        v = summed(0, h, at)
+        out_send[0, at, h * half : (h + 1) * half] = (
+            0.5 * v * (1.0 + lax.erf(v * 0.7071067811865476))).astype(BF16)
+
+    over(forward)
+    publish(0)
+    for k in (2, 1, 0):
+        out[k, col] = out_send[k]
+        pass_on(k)
+    for k in (2, 1, 0):
+        relay(k, 0).wait_send()
+        relay(k, 1).wait_send()
+        first(k, 0).wait_send()
+        first(k, 1).wait_send()
+        for which in (0, 1):
+            ref = out.at[k, diag, :, pl.ds(which * half, half)]
+            arrived(ref, g_r.at[k, 2 + which], (peer_y, peer_x)[which])
+        for s in range(6):
+            copy(k, s).wait_send()
+
+
+def middle(full, w_up, w_down):
+    _, C, tokens, _ = full.shape
+    wide = w_up.shape[1]
+    half = wide // 2
+    return pl.pallas_call(
+        middle_kernel,
+        out_shape=jax.ShapeDtypeStruct((3, C, tokens, wide), BF16),
+        in_specs=[VMEM] * 3,
+        out_specs=VMEM,
+        scratch_shapes=[
+            pltpu.VMEM((3, tokens, wide), BF16),
+            pltpu.VMEM((3, 6, tokens, half), F32), pltpu.VMEM((3, 6, tokens, half), F32),
+            pltpu.VMEM((3, 2, tokens, half), F32),
+            DMA((3, 6)), DMA((3, 6)), DMA((3, 4)), DMA((3, 4)),
+        ],
+        compiler_params=pltpu.CompilerParams(
+            collective_id=1, has_side_effects=True, vmem_limit_bytes=GRANT),
+        cost_estimate=pl.CostEstimate(flops=10**10, bytes_accessed=10**7, transcendentals=0),
+    )(full, w_up, w_down)
+
+
+def scatter_kernel(R, hidden, w_up, w_down, out, part, from_sib, from_left, from_right,
+                   sib_s, sib_r, right_s, left_s, left_r, right_r):
+    row, col = lax.axis_index("row"), lax.axis_index("col")
+    chips = R // 2
+    chip, core = row // 2, row % 2
+    sib = {"row": row + 1 - 2 * core, "col": col}
+
+    def line(step):
+        return {"row": row + 2 * step, "col": col}
+
+    greet_line(line, chip, chips, [sib])
+    rows, wide = out.shape[1], out.shape[2]
+    tile = wide // 4
+    order = []
+    low, high = 0, chips - 1
+    while low <= high:
+        order.append(high)
+        if low < high:
+            order.append(low)
+        low, high = low + 1, high - 1
+
+    def to_sib(j, z):
+        return send(part.at[j, z, 1 - core], from_sib.at[j, z], sib_s.at[j, z], sib_r.at[j, z], sib)
+
+    def to_right(j, z):
+        return send(part.at[j, z, core], from_left.at[j, z], right_s.at[j, z], left_r.at[j, z], line(1))
+
+    def to_left(j, z):
+        return send(part.at[j, z, core], from_right.at[j, z], left_s.at[j, z], right_r.at[j, z], line(-1))
+
+    def product(j, z):
+        @pl.loop(0, wide // tile)
+        def _(t):
+            at = pl.ds(pl.multiple_of(t * tile, tile), tile)
+            left = hidden[2 * j, pl.ds(z * 2 * rows, 2 * rows), :]
+            if j == 0:
+                piece = jnp.dot(left, w_down[:, at], preferred_element_type=F32)
+            else:
+                piece = lax.dot_general(left, w_up[at, :], (((1,), (1,)), ((), ())),
+                                        preferred_element_type=F32)
+            part[j, z, 0, :, at] = piece[:rows]
+            part[j, z, 1, :, at] = piece[rows:]
+        to_sib(j, z).start()
+
+    def onward(j, z):
+        to_sib(j, z).wait_recv()
+        part[j, z, core] = part[j, z, core] + from_sib[j, z]
+
+        @pl.when(z > chip)
+        def _():
+            @pl.when(chip > 0)
+            def _():
+                to_right(j, z).wait_recv()
+                part[j, z, core] = part[j, z, core] + from_left[j, z]
+
+            to_right(j, z).start()
+
+        @pl.when(z < chip)
+        def _():
+            @pl.when(chip < chips - 1)
+            def _():
+                to_left(j, z).wait_recv()
+                part[j, z, core] = part[j, z, core] + from_right[j, z]
+
+            to_left(j, z).start()
+
+    for j in (0, 1):
+        for z in order:
+            product(j, z)
+    for j in (0, 1):
+        for z in order:
+            onward(j, z)
+    for j in (0, 1):
+        out[j] = part[j, chip, core]
+
+        @pl.when(chip > 0)
+        def _():
+            to_right(j, chip).wait_recv()
+            out[j] = out[j] + from_left[j, chip]
+
+        @pl.when(chip < chips - 1)
+        def _():
+            to_left(j, chip).wait_recv()
+            out[j] = out[j] + from_right[j, chip]
+
+    for j in (0, 1):
+        for z in range(chips):
+            to_sib(j, z).wait_send()
+            pl.when(z > chip)(to_right(j, z).wait_send)
+            pl.when(z < chip)(to_left(j, z).wait_send)
+
+
+def scatter_rows(R, hidden, w_up, w_down):
+    tokens, wide = hidden.shape[1], w_up.shape[0]
+    rows, chips = tokens // R, R // 2
+    block = (2, chips, rows, wide)
+    return pl.pallas_call(
+        functools.partial(scatter_kernel, R),
+        out_shape=jax.ShapeDtypeStruct((2, rows, wide), F32),
+        in_specs=[VMEM] * 3,
+        out_specs=VMEM,
+        scratch_shapes=[pltpu.VMEM((2, chips, 2, rows, wide), F32)]
+        + [pltpu.VMEM(block, F32)] * 3 + [DMA((2, chips))] * 6,
+        compiler_params=pltpu.CompilerParams(
+            collective_id=2, has_side_effects=True, vmem_limit_bytes=GRANT),
+        cost_estimate=pl.CostEstimate(flops=10**10, bytes_accessed=10**7, transcendentals=0),
+    )(hidden, w_up, w_down)
+
+
+def final_kernel(R, C, width, gn, xb, go, gain, stats, squares, dx, g_gain, total,
+                 st_own, st_in, gp_own, gp_in, tt_own, tt_in,
+                 st_s, st_r, gp_s, gp_r, tt_s, tt_r):
+    row, col = lax.axis_index("row"), lax.axis_index("col")
+    cols = [{"row": row, "col": (col + i) % C} for i in range(1, C)]
+    rows = [{"row": (row + i) % R, "col": col} for i in range(1, R)]
+    greet(cols + rows)
+    hat, inv = normal_of(xb[...].astype(F32), stats[...], 2, width)
+    grad = gn[...]
+    scaled = grad * gain[...]
+    st_own[...] = lanes_of([jnp.sum(scaled, 1, keepdims=True), jnp.sum(scaled * hat, 1, keepdims=True)])
+    first = [send(st_own, st_in.at[i], st_s.at[i], st_r.at[i], p) for i, p in enumerate(cols)]
+    for copy in first:
+        copy.start()
+    wide = grad.shape[1]
+    gp_own[:, :wide] = jnp.broadcast_to(jnp.sum(grad * hat, 0, keepdims=True), (8, wide))
+    gp_own[:, wide:] = squares[...]
+    gp_in[row] = gp_own[...]
+    second = [send(gp_own, gp_in.at[row], gp_s.at[i], gp_r.at[i], p) for i, p in enumerate(rows)]
+    for copy in second:
+        copy.start()
+    for copy in second:
+        copy.wait()
+    gains = gp_in[0]
+    for i in range(1, R):
+        gains = gains + gp_in[i]
+    gained = gains[:, :wide]
+    g_gain[...] = gained
+    tt_own[...] = gains[:, wide:] + jnp.sum(gained * gained, 1, keepdims=True)
+    tt_in[col] = tt_own[...]
+    third = [send(tt_own, tt_in.at[col], tt_s.at[i], tt_r.at[i], p) for i, p in enumerate(cols)]
+    for copy in third:
+        copy.start()
+    for copy in first:
+        copy.wait()
+    sums = st_own[...]
+    for i in range(C - 1):
+        sums = sums + st_in[i]
+    c1, c2 = sums[:, 0:1] / width, sums[:, 1:2] / width
+    dx[...] = (go[...].astype(F32) + inv * (scaled - c1 - hat * c2)).astype(BF16)
+    for copy in third:
+        copy.wait()
+    whole = tt_in[0]
+    for i in range(1, C):
+        whole = whole + tt_in[i]
+    total[...] = whole
+
+
+def final(R, C, width, gn, x_bwd, grad_out, gain, stats, squares):
+    rows, wide = gn.shape
+    return pl.pallas_call(
+        functools.partial(final_kernel, R, C, width),
+        out_shape=(jax.ShapeDtypeStruct((rows, wide), BF16),
+                   jax.ShapeDtypeStruct((8, wide), F32),
+                   jax.ShapeDtypeStruct((8, 128), F32)),
+        in_specs=[VMEM] * 6,
+        out_specs=(VMEM, VMEM, VMEM),
+        scratch_shapes=[
+            pltpu.VMEM((rows, 128), F32), pltpu.VMEM((C - 1, rows, 128), F32),
+            pltpu.VMEM((8, wide + 128), F32), pltpu.VMEM((R, 8, wide + 128), F32),
+            pltpu.VMEM((8, 128), F32), pltpu.VMEM((C, 8, 128), F32),
+            DMA((C - 1,)), DMA((C - 1,)), DMA((R - 1,)), DMA((R - 1,)), DMA((C - 1,)), DMA((C - 1,)),
+        ],
+        compiler_params=pltpu.CompilerParams(
+            collective_id=3, has_side_effects=True, vmem_limit_bytes=GRANT),
+        cost_estimate=pl.CostEstimate(flops=10**9, bytes_accessed=10**7, transcendentals=0),
+    )(gn, x_bwd, grad_out, gain, stats, squares)
+
+
+def with_kernels(R, C):
+    def step(x_fwd, x_bwd, grad_out, gain, w_up, w_down):
+        rows, columns = x_fwd.shape
+        tokens = rows * R
+        width = columns * C
+        gain_row = gain.reshape(1, columns)
+        full, stats = gather_rows(R, C, width, x_fwd, x_bwd, grad_out, gain_row)
+        acts = middle(full.reshape(3, C, tokens // C, columns), w_up, w_down)
+        acts = acts.reshape(3, tokens, w_up.shape[1])
+        full = full.reshape(3, tokens, columns)
+        sums = scatter_rows(R, acts, w_up, w_down)
+        y_fwd = (x_fwd.astype(F32) + sums[0]).astype(BF16)
+        down_total = contract(acts[1], full[2], 0, 0)
+        up_total = contract(full[1], acts[2], 0, 0)
+        squares = jnp.sum(up_total * up_total) + jnp.sum(down_total * down_total)
+        dx, g_gain, total = final(R, C, width, sums[1], x_bwd, grad_out, gain_row, stats,
+                                  jnp.broadcast_to(squares, (8, 128)))
+        param_count = 2 * width * w_up.shape[1] * R + width
+        norm_value = jnp.sqrt(total[0, 0])
+        grad_rms = norm_value / math.sqrt(param_count)
+        factor = jnp.minimum(1.0, clip_share * math.sqrt(param_count) / norm_value)
+        return (y_fwd, dx, up_total * factor, down_total * factor, g_gain[0] * factor, grad_rms)
+
+    return step
+
+
 def solution(mesh):
     placed = (
         P("row", "col"),
@@ -123,8 +656,10 @@
         P("col", "row"),
         P("row", "col"),
     )
+    R, C = mesh.shape["row"], mesh.shape["col"]
+    body = with_kernels(R, C) if C == 4 and R % 2 == 0 else on_device
     return jax.shard_map(
-        on_device,
+        body,
         mesh=mesh,
         in_specs=placed,
         out_specs=(

time: 447 us -> 321 us (0.72)
  Pallas kernels: 0 us -> 279 us
  waiting for transfers between devices: 274 us -> 0 us
  blocking collectives: 76.2 us -> 0 us
  matrix products: 46.1 us -> 12.2 us
  between operations: 18.1 us -> 3.87 us
  other arithmetic: 29.2 us -> 15.8 us
  local copies, waits for them, and re-layouts: 1.92 us -> 9.82 us
    pallas_call x0 -> x4, Pallas kernels: none -> 279 us  [the longest x1 128 us: middle(): pl.pallas_call(middle_kernel, out_shape=jax.ShapeDtypeStruct((3, C, token...]
    reduce_scatter x4 -> x0, waiting for transfers between devices: 144 us -> none  [the longest x1 73.5 us: up_both(): lax.psum_scatter(jnp.concatenate([jnp.dot(full_a, w_up, preferred_element...]
    all_gather x6 -> x0, waiting for transfers between devices: 127 us -> none  [the longest x1 29.5 us: on_device(): pre_piece = lax.all_gather(grad_pre, 'col', axis=0, tiled=True)]
    psum x4 -> x0, blocking collectives: 76.2 us -> none  [the longest x1 38.8 us: on_device(): lax.psum(weight_squares + first_row * jnp.sum(g_gain * g_gain), ('row', '...]
    dot_general x4 -> x2, matrix products: 29.2 us -> 12.2 us  [contract(): lax.dot_general(left, right, (((left_dim,), (right_dim,)), ((), ())), pre...]
    dot_general x3 -> x0, matrix products: 17 us -> none  [the longest x1 7.12 us: on_device(): jnp.dot(lax.all_gather(hidden_a, 'col', axis=0, tiled=True), w_down, pref...]
    convert_element_type x4 -> x1, other arithmetic: 7.69 us -> 1.71 us  [step(): y_fwd = (x_fwd.astype(F32) + sums[0]).astype(BF16)]
    slice x0 -> x3, local copies, waits for them, and re-layouts: none -> 5.42 us  [the longest x2 4.24 us: step(): down_total = contract(acts[1], full[2], 0, 0)]
  transfers between devices with their start and end apart: 10 -> 0, of which waited for: 9 -> 0; matrix products, arithmetic and copies ran while one was open for 16% -> 0% of each run, Pallas kernels for 0% -> 0%
where the time goes in v1:
time: 321 us
  Pallas kernels  279 us (87%)
  other arithmetic  15.8 us (5%)
  matrix products  12.2 us (4%)
  local copies, waits for them, and re-layouts  9.82 us (3%)
  between operations  3.87 us (1%)
    pallas_call x1, Pallas kernels, middle(): pl.pallas_call(middle_kernel, out_shape=jax.ShapeDtypeStruct((3, C, token...  128 us
    pallas_call x1, Pallas kernels, scatter_rows(): pl.pallas_call(functools.partial(scatter_kernel, R), out_shape=jax.ShapeD...  86.1 us
    pallas_call x1, Pallas kernels, gather_rows(): pl.pallas_call(functools.partial(gather_kernel, R, C, width), out_shape=(...  49 us
    pallas_call x1, Pallas kernels, final(): pl.pallas_call(functools.partial(final_kernel, R, C, width), out_shape=(j...  16 us
    mul x1, other arithmetic, step(): down_total * factor  12.7 us
    dot_general x2, matrix products, contract(): lax.dot_general(left, right, (((left_dim,), (right_dim,)), ((), ())), pre...  12.2 us

profile of v1, /device:TPU:0, one launch (start us, length us, event | category | flops | bytes accessed | tf_op | source)
XLA Modules:
  0.0 321.0 jit_solution(16132315745466874406)
XLA Ops:
  0.6 1.3 reshape.39.gain
  1.9 49.0 %shard_map.109 = (bf16[3,8,64,1536]{3,2,1,0:T(8,128)(2,1)}, f32[64,128]{1,0:T(8,128)}) custom-call(bf16[64,1536]{1,0:T(8,128)(2,1)} %xa.1, bf16[64,1536]{1,0:T(8,128)(2,1)} %xb.3, bf16[64,1536]{1,0:T(8,128)(2,1)} %go.3, f32[1,1536]{1,0:T(1,128)} %reshape.39.gain), custom_call_target="tpu_custom_call" | custom-call | flops 1000000000 | bytes 10000000 | tf_op jit(solution)/shard_map/pallas_call | solution.py:274
  51.0 2.2 fusion.1
  53.1 128.2 %shard_map.110 = bf16[3,4,128,1536]{3,2,1,0:T(8,128)(2,1)} custom-call(bf16[3,4,128,1536]{3,2,1,0:T(8,128)(2,1)} %bitcast.19, bf16[1536,1536]{1,0:T(8,128)(2,1)} %w_up.3, bf16[1536,1536]{1,0:T(8,128)(2,1)} %w_down.3), custom_call_target="tpu_custom_call" | custom-call | flops 10000000000 | bytes 10000000 | tf_op jit(solution)/shard_map/pallas_call | solution.py:429
  181.4 0.0 copy-start.1
  181.4 86.1 %shard_map.111 = f32[2,64,1536]{2,1,0:T(8,128)} custom-call(bf16[3,512,1536]{2,1,0:T(8,128)(2,1)} %bitcast.18, bf16[1536,1536]{1,0:T(8,128)(2,1)} %w_up.3, bf16[1536,1536]{1,0:T(8,128)(2,1)} %w_down.3), custom_call_target="tpu_custom_call" | custom-call | flops 10000000000 | bytes 10000000 | tf_op jit(solution)/shard_map/pallas_call | solution.py:542
  267.4 0.0 copy-done.1
  267.5 1.7 fusion
  269.2 1.8 slice_bitcast_fusion.gn
  271.0 2.1 fusion.2
  273.1 6.1 %multiply_reduce_fusion.1 = (f32[]{:T(128)}, f32[1536,1536]{1,0:T(8,128)}) fusion(bf16[512,1536]{1,0:T(8,128)(2,1)S(1)} %bitcast.21, bf16[512,1536]{1,0:T(8,128)(2,1)S(1)} %bitcast.23), kind=kOutput, calls=%fused_computation.1 | convolution fusion | flops 2420637696 | bytes 12582916 | tf_op jit(solution)/shard_map/dot_general | solution.py:31
  279.1 6.1 %multiply_reduce_fusion = (f32[]{:T(128)}, f32[1536,1536]{1,0:T(8,128)}) fusion(bf16[512,1536]{1,0:T(8,128)(2,1)S(1)} %bitcast.22, bf16[512,1536]{1,0:T(8,128)(2,1)S(1)} %bitcast.20), kind=kOutput, calls=%fused_computation | convolution fusion | flops 2420637696 | bytes 12582916 | tf_op jit(solution)/shard_map/dot_general | solution.py:31
  286.5 0.6 broadcast_in_dim.3.squares
  287.1 16.0 %shard_map.112 = (bf16[64,1536]{1,0:T(8,128)(2,1)}, f32[8,1536]{1,0:T(8,128)}, f32[8,128]{1,0:T(8,128)}) custom-call(f32[64,1536]{1,0:T(8,128)} %slice_bitcast_fusion.gn, bf16[64,1536]{1,0:T(8,128)(2,1)} %xb.3, bf16[64,1536]{1,0:T(8,128)(2,1)} %go.3, f32[1,1536]{1,0:T(1,128)} %reshape.39.gain, f32[64,128]{1,0:T(8,128)} %get-tuple-element.12.stats, ...), custom_call_target="tpu_custom_call" | custom-call | flops 1000000000 | bytes 10000000 | tf_op jit(solution)/shard_map/pallas_call | solution.py:605
  303.2 1.2 slice.34
  305.1 0.0 copy-start
  305.1 12.7 %broadcast_multiply_fusion = (f32[1536,1536]{1,0:T(8,128)}, f32[1536,1536]{1,0:T(8,128)}) fusion(f32[1536,1536]{1,0:T(8,128)} %get-tuple-element.23, f32[]{:T(128)} %bitcast.8, f32[1536,1536]{1,0:T(8,128)} %get-tuple-element.21), kind=kLoop, calls=%fused_computation.2 | loop fusion | flops 4718592 | bytes 37748740 | tf_op jit(solution)/shard_map/mul | solution.py:645
  317.8 1.4 multiply_reduce_fusion.2
  319.2 0.0 copy-done
  319.2 0.7 copy.13
Async XLA Ops:
  181.4 86.1 %copy-start.1 = (bf16[64,1536]{1,0:T(8,128)(2,1)S(1)}, bf16[64,1536]{1,0:T(8,128)(2,1)}, u32[]{:S(2)}) copy-start(bf16[64,1536]{1,0:T(8,128)(2,1)} %xa.1) | copy-start | bytes 589828
  305.1 14.1 %copy-start = (bf16[64,1536]{1,0:T(8,128)(2,1)S(1)}, bf16[64,1536]{1,0:T(8,128)(2,1)}, u32[]{:S(2)}) copy-start(bf16[64,1536]{1,0:T(8,128)(2,1)} %get-tuple-element.33) | copy-start | bytes 589828

commit v2 on v1

--- a/solution.py
+++ b/solution.py
@@ -179,8 +179,11 @@
     return out
 
 
-def gather_kernel(R, C, width, xa, xb, go, gain, full, stats, st_own, st_in,
-                  st_send, st_recv, s_right, s_left, s_sib, recv):
+def layer_kernel(R, C, width, xa, xb, go, gain, w_up_hbm, w_down_hbm, full, stats, acts, sums,
+                 w_up, w_down, st_own, st_in, out_send, buf, inb, own,
+                 part, from_sib, from_left, from_right,
+                 w_sem, st_send, st_recv, s_right, s_left, s_sib, recv, sem_s, sem_r, g_s, g_r,
+                 sib_s, sib_r, right_s, left_s, left_r, right_r):
     row, col = lax.axis_index("row"), lax.axis_index("col")
     chips = R // 2
     chip, core = row // 2, row % 2
@@ -190,10 +193,25 @@
         return {"row": row + 2 * step, "col": col}
 
     cols = [{"row": row, "col": (col + i) % C} for i in range(1, C)]
+    flip_x = col + 1 - 2 * (col % 2)
+    flip_y = (col + 2) % 4
+    diag = 3 - col
+    peer_x, peer_y = {"row": row, "col": flip_x}, {"row": row, "col": flip_y}
+    share = xa.shape[0]
+    tokens, wide = out_send.shape[1], out_send.shape[2]
+    half = wide // 2
+    tile = half // 2
+    load_up = pltpu.make_async_copy(w_up_hbm, w_up, w_sem.at[0])
+    load_down = pltpu.make_async_copy(w_down_hbm, w_down, w_sem.at[1])
+    load_down.start()
+    load_up.start()
     greet_line(line, chip, chips, cols + [sib])
 
+    def block(j, owner):
+        return full.at[j, pl.ds(owner * share, share), :]
+
     def spread(j, owner, slot, src, to_right, to_left):
-        dst = full.at[j, owner]
+        dst = block(j, owner)
         out = [(None, send(src, dst, s_sib.at[j, slot], recv.at[j, owner], sib))]
         if to_right:
             out.append((chip < chips - 1,
@@ -217,18 +235,18 @@
             else:
                 pl.when(cond)(copy.wait_send)
 
-    own = {2: spread(2, row, 0, go, True, True)}
-    start(own[2])
+    mine = {2: spread(2, row, 0, go, True, True)}
+    start(mine[2])
     a, b = xa[...].astype(F32), xb[...].astype(F32)
-    sums = []
+    moments = []
     for v in (a, b):
-        sums += [jnp.sum(v, 1, keepdims=True), jnp.sum(v * v, 1, keepdims=True)]
-    st_own[...] = lanes_of(sums)
+        moments += [jnp.sum(v, 1, keepdims=True), jnp.sum(v * v, 1, keepdims=True)]
+    st_own[...] = lanes_of(moments)
     st_copies = [send(st_own, st_in.at[i], st_send.at[i], st_recv.at[i], p)
                  for i, p in enumerate(cols)]
     for copy in st_copies:
         copy.start()
-    full[2, row] = go[...]
+    block(2, row)[...] = go[...]
     for copy in st_copies:
         copy.wait()
     total = st_own[...]
@@ -237,27 +255,12 @@
     stats[...] = total
     for j, x, at in ((1, xb, 2), (0, xa, 0)):
         hat, _ = normal_of(x[...].astype(F32), total, at, width)
-        full[j, row] = (hat * gain[...]).astype(BF16)
-        own[j] = spread(j, row, 0, full.at[j, row], True, True)
-        start(own[j])
-    for step in range(1, chips):
-        for j in (2, 1, 0):
-            for sign in (-1, 1):
-                ok = chip >= step if sign < 0 else chip + step < chips
-
-                @pl.when(ok)
-                def _():
-                    owner = row + 2 * sign * step
-                    arrived(full.at[j, owner], recv.at[j, owner], line(sign))
-                    slot = step if sign < 0 else chips - 1 + step
-                    start(spread(j, owner, slot, full.at[j, owner], sign < 0, sign > 0))
-    for j in (2, 1, 0):
-        finish(own[j])
-        for chip_of in range(chips):
-            owner = 2 * chip_of + 1 - core
-            arrived(full.at[j, owner], recv.at[j, owner], sib)
-    for step in range(1, chips):
-        for j in (2, 1, 0):
+        block(j, row)[...] = (hat * gain[...]).astype(BF16)
+        mine[j] = spread(j, row, 0, block(j, row), True, True)
+        start(mine[j])
+
+    def relays(j, visit):
+        for step in range(1, chips):
             for sign in (-1, 1):
                 ok = chip >= step if sign < 0 else chip + step < chips
 
@@ -265,45 +268,23 @@
                 def _():
                     owner = row + 2 * sign * step
                     slot = step if sign < 0 else chips - 1 + step
-                    finish(spread(j, owner, slot, full.at[j, owner], sign < 0, sign > 0))
-
-
-def gather_rows(R, C, width, x_fwd, x_bwd, grad_out, gain):
-    rows, columns = x_fwd.shape
-    slots = 2 * (R // 2) - 1
-    return pl.pallas_call(
-        functools.partial(gather_kernel, R, C, width),
-        out_shape=(jax.ShapeDtypeStruct((3, R, rows, columns), BF16),
-                   jax.ShapeDtypeStruct((rows, 128), F32)),
-        in_specs=[VMEM] * 4,
-        out_specs=(VMEM, VMEM),
-        scratch_shapes=[
-            pltpu.VMEM((rows, 128), F32), pltpu.VMEM((C - 1, rows, 128), F32),
-            DMA((C - 1,)), DMA((C - 1,)),
-            DMA((3, slots)), DMA((3, slots)), DMA((3, slots)), DMA((3, R)),
-        ],
-        compiler_params=pltpu.CompilerParams(
-            collective_id=0, has_side_effects=True, vmem_limit_bytes=GRANT),
-        cost_estimate=pl.CostEstimate(flops=10**9, bytes_accessed=10**7, transcendentals=0),
-    )(x_fwd, x_bwd, grad_out, gain)
-
-
-def middle_kernel(full, w_up, w_down, out, out_send, buf, inb, own, sem_s, sem_r, g_s, g_r):
-    row, col = lax.axis_index("row"), lax.axis_index("col")
-    flip_x = col + 1 - 2 * (col % 2)
-    flip_y = (col + 2) % 4
-    diag = 3 - col
-    peer_x, peer_y = {"row": row, "col": flip_x}, {"row": row, "col": flip_y}
-    greet([peer_x, peer_y])
-    tokens, wide = out.shape[2], out.shape[3]
-    half = wide // 2
-    tile = half // 2
-
-    def part(j, q, put):
+                    visit(owner, sign, spread(j, owner, slot, block(j, owner), sign < 0, sign > 0))
+
+    def gathered(j):
+        def visit(owner, sign, copies):
+            arrived(block(j, owner), recv.at[j, owner], line(sign))
+            start(copies)
+
+        relays(j, visit)
+        for chip_of in range(chips):
+            owner = 2 * chip_of + 1 - core
+            arrived(block(j, owner), recv.at[j, owner], sib)
+
+    def multiply(j, q, put):
         @pl.loop(0, wide // tile)
         def _(t):
             at = pl.ds(pl.multiple_of(t * tile, tile), tile)
-            left = full[j, q]
+            left = full[j, pl.ds(q * tokens, tokens), :]
             if j == 2:
                 piece = lax.dot_general(left, w_down[at, :], (((1,), (1,)), ((), ())),
                                         preferred_element_type=F32)
@@ -323,30 +304,30 @@
 
     target = (peer_x, peer_y, peer_x, peer_x, peer_y, peer_y)
 
-    def copy(j, s):
+    def hop(j, s):
         return send(buf.at[j, s], inb.at[j, s], sem_s.at[j, s], sem_r.at[j, s], target[s])
 
     def products(j):
-        part(j, diag, into(j, 0))
-        copy(j, 0).start()
-        copy(j, 1).start()
-        part(j, flip_x, into(j, 2))
-        copy(j, 2).start()
-        part(j, flip_y, into(j, 4))
-        copy(j, 5).start()
-        part(j, col, keep(j))
+        multiply(j, diag, into(j, 0))
+        hop(j, 0).start()
+        hop(j, 1).start()
+        multiply(j, flip_x, into(j, 2))
+        hop(j, 2).start()
+        multiply(j, flip_y, into(j, 4))
+        hop(j, 5).start()
+        multiply(j, col, keep(j))
 
     def transit(j):
-        copy(j, 0).wait_recv()
+        hop(j, 0).wait_recv()
         buf[j, 4] = buf[j, 4] + inb[j, 0]
-        copy(j, 4).start()
-        copy(j, 1).wait_recv()
+        hop(j, 4).start()
+        hop(j, 1).wait_recv()
         buf[j, 3] = buf[j, 3] + inb[j, 1]
-        copy(j, 3).start()
-
-    def total(j):
+        hop(j, 3).start()
+
+    def landed(j):
         for s in range(2, 6):
-            copy(j, s).wait_recv()
+            hop(j, s).wait_recv()
 
     def summed(j, h, at):
         return own[j, h, at, :] + inb[j, 2 + h, at, :] + inb[j, 4 + h, at, :]
@@ -361,11 +342,11 @@
 
     def first(k, which):
         peer = (peer_x, peer_y)[which]
-        return send(out_send.at[k], out.at[k, col], g_s.at[k, which], g_r.at[k, which], peer)
+        return send(out_send.at[k], acts.at[k, pl.ds(col * tokens, tokens), :], g_s.at[k, which], g_r.at[k, which], peer)
 
     def relay(k, which):
         owner = (flip_x, flip_y)[which]
-        ref = out.at[k, owner, :, pl.ds(which * half, half)]
+        ref = acts.at[k, pl.ds(owner * tokens, tokens), pl.ds(which * half, half)]
         return send(ref, ref, g_s.at[k, 2 + which], g_r.at[k, 2 + which], (peer_y, peer_x)[which])
 
     def publish(k):
@@ -377,14 +358,6 @@
         relay(k, 0).start()
         first(k, 1).wait_recv()
         relay(k, 1).start()
-
-    products(2)
-    products(1)
-    transit(2)
-    products(0)
-    transit(1)
-    total(2)
-    total(1)
 
     def backward(h, at):
         v = summed(1, h, at)
@@ -394,68 +367,13 @@
         out_send[1, at, h * half : (h + 1) * half] = (v * phi).astype(BF16)
         out_send[2, at, h * half : (h + 1) * half] = (g * slope).astype(BF16)
 
-    over(backward)
-    transit(0)
-    publish(2)
-    publish(1)
-    total(0)
-
     def forward(h, at):
         v = summed(0, h, at)
         out_send[0, at, h * half : (h + 1) * half] = (
             0.5 * v * (1.0 + lax.erf(v * 0.7071067811865476))).astype(BF16)
 
-    over(forward)
-    publish(0)
-    for k in (2, 1, 0):
-        out[k, col] = out_send[k]
-        pass_on(k)
-    for k in (2, 1, 0):
-        relay(k, 0).wait_send()
-        relay(k, 1).wait_send()
-        first(k, 0).wait_send()
-        first(k, 1).wait_send()
-        for which in (0, 1):
-            ref = out.at[k, diag, :, pl.ds(which * half, half)]
-            arrived(ref, g_r.at[k, 2 + which], (peer_y, peer_x)[which])
-        for s in range(6):
-            copy(k, s).wait_send()
-
-
-def middle(full, w_up, w_down):
-    _, C, tokens, _ = full.shape
-    wide = w_up.shape[1]
-    half = wide // 2
-    return pl.pallas_call(
-        middle_kernel,
-        out_shape=jax.ShapeDtypeStruct((3, C, tokens, wide), BF16),
-        in_specs=[VMEM] * 3,
-        out_specs=VMEM,
-        scratch_shapes=[
-            pltpu.VMEM((3, tokens, wide), BF16),
-            pltpu.VMEM((3, 6, tokens, half), F32), pltpu.VMEM((3, 6, tokens, half), F32),
-            pltpu.VMEM((3, 2, tokens, half), F32),
-            DMA((3, 6)), DMA((3, 6)), DMA((3, 4)), DMA((3, 4)),
-        ],
-        compiler_params=pltpu.CompilerParams(
-            collective_id=1, has_side_effects=True, vmem_limit_bytes=GRANT),
-        cost_estimate=pl.CostEstimate(flops=10**10, bytes_accessed=10**7, transcendentals=0),
-    )(full, w_up, w_down)
-
-
-def scatter_kernel(R, hidden, w_up, w_down, out, part, from_sib, from_left, from_right,
-                   sib_s, sib_r, right_s, left_s, left_r, right_r):
-    row, col = lax.axis_index("row"), lax.axis_index("col")
-    chips = R // 2
-    chip, core = row // 2, row % 2
-    sib = {"row": row + 1 - 2 * core, "col": col}
-
-    def line(step):
-        return {"row": row + 2 * step, "col": col}
-
-    greet_line(line, chip, chips, [sib])
-    rows, wide = out.shape[1], out.shape[2]
-    tile = wide // 4
+    rows, broad = sums.shape[1], sums.shape[2]
+    step_n = broad // 4
     order = []
     low, high = 0, chips - 1
     while low <= high:
@@ -474,10 +392,10 @@
         return send(part.at[j, z, core], from_right.at[j, z], left_s.at[j, z], right_r.at[j, z], line(-1))
 
     def product(j, z):
-        @pl.loop(0, wide // tile)
+        @pl.loop(0, broad // step_n)
         def _(t):
-            at = pl.ds(pl.multiple_of(t * tile, tile), tile)
-            left = hidden[2 * j, pl.ds(z * 2 * rows, 2 * rows), :]
+            at = pl.ds(pl.multiple_of(t * step_n, step_n), step_n)
+            left = acts[2 * j, pl.ds(z * 2 * rows, 2 * rows), :]
             if j == 0:
                 piece = jnp.dot(left, w_down[:, at], preferred_element_type=F32)
             else:
@@ -509,24 +427,66 @@
 
             to_left(j, z).start()
 
+
+    def complete(k):
+        for which in (0, 1):
+            ref = acts.at[k, pl.ds(diag * tokens, tokens), pl.ds(which * half, half)]
+            arrived(ref, g_r.at[k, 2 + which], (peer_y, peer_x)[which])
+
+    gathered(2)
+    load_down.wait()
+    products(2)
+    gathered(1)
+    load_up.wait()
+    products(1)
+    transit(2)
+    gathered(0)
+    products(0)
+    transit(1)
+    landed(2)
+    landed(1)
+    transit(0)
+    over(backward)
+    publish(2)
+    landed(0)
+    over(forward)
+    publish(0)
+    for k in (2, 0, 1):
+        acts[k, pl.ds(col * tokens, tokens), :] = out_send[k]
+    pass_on(2)
+    publish(1)
+    complete(2)
+    for z in order:
+        product(1, z)
+    pass_on(0)
+    complete(0)
+    for z in order:
+        onward(1, z)
+        product(0, z)
+    pass_on(1)
+    for z in order:
+        onward(0, z)
+    complete(1)
+    for j in (2, 1, 0):
+        finish(mine[j])
+        relays(j, lambda owner, sign, copies: finish(copies))
+        for which in (0, 1):
+            relay(j, which).wait_send()
+            first(j, which).wait_send()
+        for s in range(6):
+            hop(j, s).wait_send()
     for j in (0, 1):
-        for z in order:
-            product(j, z)
-    for j in (0, 1):
-        for z in order:
-            onward(j, z)
-    for j in (0, 1):
-        out[j] = part[j, chip, core]
+        sums[j] = part[j, chip, core]
 
         @pl.when(chip > 0)
         def _():
             to_right(j, chip).wait_recv()
-            out[j] = out[j] + from_left[j, chip]
+            sums[j] = sums[j] + from_left[j, chip]
 
         @pl.when(chip < chips - 1)
         def _():
             to_left(j, chip).wait_recv()
-            out[j] = out[j] + from_right[j, chip]
+            sums[j] = sums[j] + from_right[j, chip]
 
     for j in (0, 1):
         for z in range(chips):
@@ -535,21 +495,38 @@
             pl.when(z < chip)(to_left(j, z).wait_send)
 
 
-def scatter_rows(R, hidden, w_up, w_down):
-    tokens, wide = hidden.shape[1], w_up.shape[0]
-    rows, chips = tokens // R, R // 2
-    block = (2, chips, rows, wide)
+def layer(R, C, width, x_fwd, x_bwd, grad_out, gain, w_up, w_down):
+    rows, columns = x_fwd.shape
+    wide = w_up.shape[1]
+    chips, slots = R // 2, 2 * (R // 2) - 1
+    count = rows * R
+    tokens, half = count // C, wide // 2
+    line_block = (2, chips, rows, columns)
     return pl.pallas_call(
-        functools.partial(scatter_kernel, R),
-        out_shape=jax.ShapeDtypeStruct((2, rows, wide), F32),
-        in_specs=[VMEM] * 3,
-        out_specs=VMEM,
-        scratch_shapes=[pltpu.VMEM((2, chips, 2, rows, wide), F32)]
-        + [pltpu.VMEM(block, F32)] * 3 + [DMA((2, chips))] * 6,
+        functools.partial(layer_kernel, R, C, width),
+        out_shape=(jax.ShapeDtypeStruct((3, count, columns), BF16),
+                   jax.ShapeDtypeStruct((rows, 128), F32),
+                   jax.ShapeDtypeStruct((3, count, wide), BF16),
+                   jax.ShapeDtypeStruct((2, rows, columns), F32)),
+        in_specs=[VMEM] * 4 + [pl.BlockSpec(memory_space=pl.ANY)] * 2,
+        out_specs=(VMEM,) * 4,
+        scratch_shapes=[
+            pltpu.VMEM(w_up.shape, BF16), pltpu.VMEM(w_down.shape, BF16),
+            pltpu.VMEM((rows, 128), F32), pltpu.VMEM((C - 1, rows, 128), F32),
+            pltpu.VMEM((3, tokens, wide), BF16),
+            pltpu.VMEM((3, 6, tokens, half), F32), pltpu.VMEM((3, 6, tokens, half), F32),
+            pltpu.VMEM((3, 2, tokens, half), F32),
+            pltpu.VMEM((2, chips, 2, rows, columns), F32),
+        ]
+        + [pltpu.VMEM(line_block, F32)] * 3
+        + [DMA((2,)), DMA((C - 1,)), DMA((C - 1,)),
+           DMA((3, slots)), DMA((3, slots)), DMA((3, slots)), DMA((3, R)),
+           DMA((3, 6)), DMA((3, 6)), DMA((3, 4)), DMA((3, 4))]
+        + [DMA((2, chips))] * 6,
         compiler_params=pltpu.CompilerParams(
-            collective_id=2, has_side_effects=True, vmem_limit_bytes=GRANT),
+            collective_id=0, has_side_effects=True, vmem_limit_bytes=GRANT),
         cost_estimate=pl.CostEstimate(flops=10**10, bytes_accessed=10**7, transcendentals=0),
-    )(hidden, w_up, w_down)
+    )(x_fwd, x_bwd, grad_out, gain, w_up, w_down)
 
 
 def final_kernel(R, C, width, gn, xb, go, gain, stats, squares, dx, g_gain, total,
@@ -624,14 +601,9 @@
 def with_kernels(R, C):
     def step(x_fwd, x_bwd, grad_out, gain, w_up, w_down):
         rows, columns = x_fwd.shape
-        tokens = rows * R
         width = columns * C
         gain_row = gain.reshape(1, columns)
-        full, stats = gather_rows(R, C, width, x_fwd, x_bwd, grad_out, gain_row)
-        acts = middle(full.reshape(3, C, tokens // C, columns), w_up, w_down)
-        acts = acts.reshape(3, tokens, w_up.shape[1])
-        full = full.reshape(3, tokens, columns)
-        sums = scatter_rows(R, acts, w_up, w_down)
+        full, stats, acts, sums = layer(R, C, width, x_fwd, x_bwd, grad_out, gain_row, w_up, w_down)
         y_fwd = (x_fwd.astype(F32) + sums[0]).astype(BF16)
         down_total = contract(acts[1], full[2], 0, 0)
         up_total = contract(full[1], acts[2], 0, 0)

time: 321 us -> 276 us (0.86)
  Pallas kernels: 279 us -> 232 us
  matrix products: 12.2 us -> 17.7 us
  local copies, waits for them, and re-layouts: 9.82 us -> 5.53 us
    pallas_call x3 -> x1, Pallas kernels: 263 us -> 216 us  [layer(): pl.pallas_call(functools.partial(layer_kernel, R, C, width), out_shape=(j...]
    dot_general x2, matrix products: 12.2 us -> 17.7 us  [contract(): lax.dot_general(left, right, (((left_dim,), (right_dim,)), ((), ())), pre...]
    slice x2 -> x0, local copies, waits for them, and re-layouts: 4.24 us -> none  [step(): down_total = contract(acts[1], full[2], 0, 0)]
where the time goes in v2:
time: 276 us; the launch traced here: 275 us
  Pallas kernels  232 us (84%)
  matrix products  17.7 us (6%)
  other arithmetic  15.8 us (6%)
  local copies, waits for them, and re-layouts  5.53 us (2%)
  between operations  3.83 us (1%)
    pallas_call x1, Pallas kernels, layer(): pl.pallas_call(functools.partial(layer_kernel, R, C, width), out_shape=(j...  216 us
    dot_general x2, matrix products, contract(): lax.dot_general(left, right, (((left_dim,), (right_dim,)), ((), ())), pre...  17.7 us
    pallas_call x1, Pallas kernels, final(): pl.pallas_call(functools.partial(final_kernel, R, C, width), out_shape=(j...  16 us
    mul x1, other arithmetic, step(): down_total * factor  12.7 us

profile of v2, /device:TPU:0, one launch (start us, length us, event | category | flops | bytes accessed | tf_op | source)
XLA Modules:
  0.0 275.3 jit_solution(7247534866105118429)
XLA Ops:
  0.6 1.3 reshape.24.gain
  1.9 0.0 copy-start.1
  1.9 216.4 %shard_map.109 = (bf16[3,512,1536]{2,1,0:T(8,128)(2,1)}, f32[64,128]{1,0:T(8,128)}, bf16[3,512,1536]{2,1,0:T(8,128)(2,1)}, f32[2,64,1536]{2,1,0:T(8,128)}) custom-call(bf16[64,1536]{1,0:T(8,128)(2,1)} %xa.1, bf16[64,1536]{1,0:T(8,128)(2,1)} %xb.3, bf16[64,1536]{1,0:T(8,128)(2,1)} %go.3, f32[1,1536]{1,0:T(1,128)} %reshape.24.gain, ...), custom_call_target="tpu_custom_call" | custom-call | flops 10000000000 | bytes 10000000 | tf_op jit(solution)/shard_map/pallas_call | solution.py:505
  218.3 0.0 copy-done.1
  218.3 1.7 fusion.10
  220.0 1.8 slice_bitcast_fusion.gn
  221.8 8.9 %multiply_reduce_fusion = (f32[]{:T(128)}, f32[1536,1536]{1,0:T(8,128)}) fusion(bf16[3,512,1536]{2,1,0:T(8,128)(2,1)} %get-tuple-element.15, bf16[3,512,1536]{2,1,0:T(8,128)(2,1)} %get-tuple-element.16), kind=kOutput, calls=%fused_computation | convolution fusion | flops 2420637696 | bytes 12582916 | tf_op jit(solution)/shard_map/dot_general | solution.py:31
  230.7 8.9 %multiply_reduce_fusion.1 = (f32[]{:T(128)}, f32[1536,1536]{1,0:T(8,128)}) fusion(bf16[3,512,1536]{2,1,0:T(8,128)(2,1)} %get-tuple-element.16, bf16[3,512,1536]{2,1,0:T(8,128)(2,1)} %get-tuple-element.15), kind=kOutput, calls=%fused_computation.1 | convolution fusion | flops 2420637696 | bytes 12582916 | tf_op jit(solution)/shard_map/dot_general | solution.py:31
  240.8 0.6 broadcast_in_dim.3.squares
  241.4 16.0 %shard_map.110 = (bf16[64,1536]{1,0:T(8,128)(2,1)}, f32[8,1536]{1,0:T(8,128)}, f32[8,128]{1,0:T(8,128)}) custom-call(f32[64,1536]{1,0:T(8,128)} %slice_bitcast_fusion.gn, bf16[64,1536]{1,0:T(8,128)(2,1)} %xb.3, bf16[64,1536]{1,0:T(8,128)(2,1)} %go.3, f32[1,1536]{1,0:T(1,128)} %reshape.24.gain, f32[64,128]{1,0:T(8,128)} %get-tuple-element.14.stats, ...), custom_call_target="tpu_custom_call" | custom-call | flops 1000000000 | bytes 10000000 | tf_op jit(solution)/shard_map/pallas_call | solution.py:582
  257.4 1.2 slice.30
  259.4 0.0 copy-start
  259.4 12.7 %broadcast_multiply_fusion = (f32[1536,1536]{1,0:T(8,128)}, f32[1536,1536]{1,0:T(8,128)}) fusion(f32[1536,1536]{1,0:T(8,128)} %get-tuple-element.23, f32[]{:T(128)} %bitcast.6, f32[1536,1536]{1,0:T(8,128)} %get-tuple-element.21), kind=kLoop, calls=%fused_computation.2 | loop fusion | flops 4718592 | bytes 37748740 | tf_op jit(solution)/shard_map/mul | solution.py:617
  272.1 1.4 multiply_reduce_fusion.2
  273.5 0.0 copy-done
  273.5 0.7 copy.13
Async XLA Ops:
  1.9 216.4 %copy-start.1 = (bf16[64,1536]{1,0:T(8,128)(2,1)S(1)}, bf16[64,1536]{1,0:T(8,128)(2,1)}, u32[]{:S(2)}) copy-start(bf16[64,1536]{1,0:T(8,128)(2,1)} %xa.1) | copy-start | bytes 589828
  259.4 14.1 %copy-start = (bf16[64,1536]{1,0:T(8,128)(2,1)S(1)}, bf16[64,1536]{1,0:T(8,128)(2,1)}, u32[]{:S(2)}) copy-start(bf16[64,1536]{1,0:T(8,128)(2,1)} %get-tuple-element.33) | copy-start | bytes 589828
